TPU v7x, 32 devices: a whole 2x2x4 slice. The times are simulated.
32 devices in a mesh: grp: 2 (over y), dp: 16 (over z, x, core).
Axes of the slice: x: 2, y: 2, z: 4, core: 2. Of those that a mesh axis runs over, the one named last changes fastest.
Arguments:
- params: float32 [1900544], P(('grp', 'dp')), parts along dimension 0, may hold values from -0.3 to 0.3
- momentum: float32 [1900544], P(('grp', 'dp')), parts along dimension 0, may hold values from -6 to 6
- noise_draws: float32 [2, 950272], P('grp', 'dp'), parts along dimension 0, may hold values from -6 to 6
- images: float32 [16384, 448], P(('grp', 'dp')), parts along dimension 0, may hold values from -6 to 6
- labels: int32 [16384], P(('grp', 'dp')), parts along dimension 0, may hold values from 0 to 9
- indices: int32 [2, 4096], P('grp', 'dp'), parts along dimension 0, may hold values from 0 to 511
Outputs:
- params_out: float32 [1900544], P(('grp', 'dp')), parts along dimension 0
- momentum_out: float32 [1900544], P(('grp', 'dp')), parts along dimension 0
- losses: float32 [2], P('grp'), parts along dimension 0
There are 2 independent parts, one for each index of `grp`. A program takes and returns all parts, laid end to end along the dimension named above; each array names one. Nothing has to cross between parts.
All inputs are finite; a program needn't handle non-finite values.
Results may differ from a plain program's by a relative error of at most 0.0003.
Values sent between devices are 32-bit elements; how exact they have to be, the bound alone decides.
A program may use at most 64 MiB of HBM per device.

v0:
```python
import math
import jax
import jax.numpy as jnp
from jax import lax
from jax.sharding import PartitionSpec as P

DIN = 448
H = 2048
OUT = 10
step_size = 0.02
friction = 15.0


def unpack(flat_vec):
    in_end = DIN * H
    w_in = flat_vec[:in_end].reshape(DIN, H)
    b_in = flat_vec[in_end : in_end + H]
    hid_end = in_end + H
    w_out = flat_vec[hid_end : hid_end + H * OUT].reshape(H, OUT)
    b_out = flat_vec[hid_end + H * OUT : hid_end + H * OUT + OUT]
    return (w_in, b_in, w_out, b_out)


def total_nll(flat_vec, chosen_rows, targets):
    w_in, b_in, w_out, b_out = unpack(flat_vec)
    hidden = jnp.tanh(
        jnp.dot(
            chosen_rows, w_in, precision=lax.Precision.HIGHEST, preferred_element_type=jnp.float32
        )
        + b_in
    )
    logits = (
        jnp.dot(hidden, w_out, precision=lax.Precision.HIGHEST, preferred_element_type=jnp.float32)
        + b_out
    )
    log_norm = jnp.log(jnp.sum(jnp.exp(logits), axis=1))
    classes = lax.broadcasted_iota(jnp.int32, logits.shape, 1)
    picked = jnp.sum(jnp.where(targets[:, None] == classes, logits, 0.0), axis=1)
    return jnp.sum(log_norm - picked)


def prior_precision(flat_index):
    in_end = DIN * H
    hid_end = in_end + H
    out_end = hid_end + H * OUT
    return jnp.where(
        flat_index < in_end,
        float(DIN),
        jnp.where(flat_index < hid_end, 1.0, jnp.where(flat_index < out_end, float(H), 1.0)),
    )


def body(params, momentum, noise_draws, images, labels, indices):
    shard_len = params.shape[0]
    shard_start = lax.axis_index("dp") * shard_len
    precision = prior_precision(shard_start + lax.iota(jnp.int32, shard_len))
    scale_data = images.shape[0] / indices.shape[1]
    row_count = lax.axis_size("dp") * indices.shape[1]
    gathered = lax.all_gather(params, "dp", axis=0, tiled=True)
    picked_rows = indices[0]
    chosen_rows = jnp.take(images, picked_rows, axis=0)
    targets = jnp.take(labels, picked_rows, axis=0)
    nll_part, pullback = jax.vjp(
        lambda weights_flat: total_nll(weights_flat, chosen_rows, targets), gathered
    )
    (local_grad,) = pullback(jnp.ones_like(nll_part))
    losses = [lax.psum(nll_part, "dp") / row_count]
    summed = lax.psum(local_grad, "dp")
    own_grad = lax.dynamic_slice_in_dim(summed, shard_start, shard_len)
    total_force = scale_data * own_grad + precision * params
    momentum = (
        (1.0 - step_size * friction) * momentum
        - step_size * total_force
        + math.sqrt(2.0 * friction * step_size) * noise_draws[0]
    )
    params = params + step_size * momentum
    return (params, momentum, jnp.stack(losses))


def solution(mesh):
    placed = (
        P(("grp", "dp")),
        P(("grp", "dp")),
        P("grp", "dp"),
        P(("grp", "dp"), None),
        P(("grp", "dp")),
        P("grp", "dp"),
    )
    return jax.shard_map(
        body,
        mesh=mesh,
        in_specs=placed,
        out_specs=(P(("grp", "dp")), P(("grp", "dp")), P("grp")),
        check_vma=False,
    )
```

profile of v0, /device:TPU:0, one launch (start us, length us, event | category | flops | bytes accessed | tf_op | source)
XLA Modules:
  0.0 212.2 jit_solution(1588823697586954154)
XLA Ops:
  7.2 0.0 copy-start
  7.2 0.0 copy-start.5
  7.2 0.0 all-gather.2.cloned.1.call-start
  7.2 0.7 all-gather.2.cloned.1.call-update
  7.9 0.0 all-reduce.6.cloned.1.call-start
  8.0 1.5 copy.12
  9.5 0.0 copy-done.5
  9.5 0.0 copy-done
  9.5 1.9 gather_fusion
  11.5 1.0 gather_fusion.1
  12.5 48.9 %all-gather.2.cloned.1.call-done = f32[950272]{0:T(1024)} async-done(((f32[59392]{0:T(1024)}), f32[950272]{0:T(1024)}) %all-gather.2.cloned.1.call-update) | async-done | bytes 3801104 | tf_op jit(solution)/shard_map/all_gather | solution.py:59
  61.4 4.1 %slice.31 = f32[917504]{0:T(1024)} slice(f32[950272]{0:T(1024)} %all-gather.2.cloned.1.call-done), slice={[0:917504]} | slice | bytes 7340032 | tf_op jit(solution)/shard_map/jvp()/slice | solution.py:16
  65.5 4.8 %slice.23 = f32[448,2048]{1,0:T(8,128)} reshape(f32[917504]{0:T(1024)} %slice.31) | data formatting | bytes 7340032 | tf_op jit(solution)/shard_map/jvp()/slice | solution.py:16
  70.3 1.0 reshape.81
  71.3 0.0 slice-start.2
  71.3 5.7 %fusion = f32[256,2048]{1,0:T(8,128)S(1)} fusion(f32[448,2048]{1,0:T(8,128)} %slice.23, f32[2048]{0:T(1024)S(1)} %slice-done.1, f32[256,448]{1,0:T(8,128)S(1)} %gather_fusion.1, pred[256]{0:T(512)(128)(4,1)S(1)} %get-tuple-element.8), kind=kOutput, calls=%fused_computation.4 | convolution fusion | flops 2819211264 | bytes 6234368 | tf_op jit(solution)/shard_map/jvp()/dot_general | solution.py:27
  77.1 0.0 slice-done.2
  77.1 1.9 exponential_reduce_fusion
  78.9 0.1 select_reduce_fusion
  79.1 4.5 %fusion.10 = f32[2048,10]{1,0:T(8,128)} fusion(f32[256,2048]{1,0:T(8,128)S(1)} %fusion, f32[256,10]{0,1:T(8,128)S(1)} %get-tuple-element.10, f32[256]{0:T(256)S(1)} %broadcast_divide_fusion, s32[256]{0:T(256)S(1)} %get-tuple-element.7), kind=kOutput, calls=%fused_computation.26 | convolution fusion | flops 62924800 | bytes 2191360 | tf_op jit(solution)/shard_map/transpose(jvp())/dot_general | solution.py:33
  83.6 2.1 fusion.18
  85.7 2.0 reshape.82
  87.7 4.7 %convolution_bitcast_fusion = f32[56,16,8,128]{3,2,1,0:T(8,128)S(1)} fusion(f32[256,2048]{1,0:T(8,128)S(1)} %get-tuple-element.12, f32[256,448]{1,0:T(8,128)} %copy-done.1, pred[256]{0:T(512)(128)(4,1)S(1)} %get-tuple-element.8), kind=kOutput, calls=%fused_computation.6 | convolution fusion | flops 2818686976 | bytes 6226176 | tf_op jit(solution)/shard_map/transpose(jvp())/dot_general | solution.py:27
  92.4 0.8 copy.15
  93.2 2.1 %pad_add_fusion = f32[950272]{0:T(1024)} fusion(f32[917504]{0:T(1024)S(1)} %bitcast.15, f32[2048]{0:T(1024)S(1)} %get-tuple-element.11, f32[20480]{0:T(1024)S(1)} %reshape.82, f32[10]{0:T(128)S(1)} %get-tuple-element.4), kind=kLoop, calls=%fused_computation.2 | loop fusion | flops 2850816 | bytes 7561256 | tf_op jit(solution)/shard_map/transpose(jvp())/add_any | solution.py:16
  95.3 0.0 all-reduce.6.cloned.1.call-update
  95.3 0.9 copy-done.4
  96.2 0.2 broadcast_multiply_fusion
  96.5 0.6 subtract_reduce_fusion
  97.1 32.9 %psum.15 = f32[]{:T(128)} all-reduce(f32[]{:T(128)} %subtract_reduce_fusion), channel_id=1, replica_groups=mesh['grp'=2,'dp'=16] {'dp'}, use_global_device_ids=true, to_apply=%region_6.7 | all-reduce | flops 1 | bytes 8 | tf_op jit(solution)/shard_map/psum | solution.py:67
  130.7 71.6 %all-reduce.6.cloned.1.call-done = f32[950272]{0:T(1024)} async-done(((f32[950272]{0:T(1024)}), f32[950272]{0:T(1024)}) %all-reduce.6.cloned.1.call-update) | async-done | bytes 3801104 | tf_op jit(solution)/shard_map/psum | solution.py:68
  202.3 1.9 multiply_add_fusion
  (15 shorter events, 0.0 us)
Async XLA Ops:
  7.2 2.4 %copy-start = (s32[512]{0:T(512)S(1)}, s32[512]{0:T(512)}, u32[]{:S(2)}) copy-start(s32[512]{0:T(512)} %param.10) | copy-start | bytes 6148
  7.2 2.3 %copy-start.5 = (s32[1,256]{1,0:T(1,128)S(1)}, s32[1,256]{1,0:T(1,128)}, u32[]{:S(2)}) copy-start(s32[1,256]{1,0:T(1,128)} %param.11) | copy-start | bytes 3076
  7.2 54.2 %all-gather.2.cloned.1.call-start = ((), (), s32[]{:S(2)}) async-start(), calls=%async_computation | async-start | bytes 4038656 | tf_op jit(solution)/shard_map/all_gather | solution.py:59
  7.9 194.4 %all-reduce.6.cloned.1.call-start = ((), (), s32[]{:S(2)}) async-start(), calls=%async_computation.1 | async-start | bytes 7602176 | tf_op jit(solution)/shard_map/psum | solution.py:68
  12.5 58.9 %copy-start.1 = (f32[256,448]{1,0:T(8,128)}, f32[256,448]{1,0:T(8,128)S(1)}, u32[]{:S(2)}) copy-start(f32[256,448]{1,0:T(8,128)S(1)} %gather_fusion.1) | copy-start | bytes 1376260
  65.5 4.8 %slice-start = ((f32[950272]{0:T(1024)}), f32[20480]{0:T(1024)S(1)}, s32[]{:S(2)}) async-start(f32[950272]{0:T(1024)} %all-gather.2.cloned.1.call-done), calls=%async_computation.2 | async-start | bytes 163840 | tf_op jit(solution)/shard_map/jvp()/slice | solution.py:19
  65.5 5.8 %slice-start.1 = ((f32[950272]{0:T(1024)}), f32[2048]{0:T(1024)S(1)}, s32[]{:S(2)}) async-start(f32[950272]{0:T(1024)} %all-gather.2.cloned.1.call-done), calls=%async_computation.3 | async-start | bytes 16384 | tf_op jit(solution)/shard_map/jvp()/slice | solution.py:17
  71.3 5.7 %slice-start.2 = ((f32[950272]{0:T(1024)}), f32[10]{0:T(128)S(1)}, s32[]{:S(2)}) async-start(f32[950272]{0:T(1024)} %all-gather.2.cloned.1.call-done), calls=%async_computation.4 | async-start | bytes 1024 | tf_op jit(solution)/shard_map/jvp()/slice | solution.py:20
  95.3 0.9 copy-start.4
  95.3 107.0 %copy-start.2 = (f32[59392]{0:T(1024)S(1)}, f32[59392]{0:T(1024)}, u32[]{:S(2)}) copy-start(f32[59392]{0:T(1024)} %param.6) | copy-start | bytes 712708
  95.3 107.0 %copy-start.3 = (f32[59392]{0:T(1024)S(1)}, f32[59392]{0:T(1024)}, u32[]{:S(2)}) copy-start(f32[59392]{0:T(1024)} %param.7) | copy-start | bytes 712708
Sparse Core Ops, SparseCore 0:
  10.3 51.0 all-gather.1
  95.5 106.8 all-reduce.5
where the time goes:
time: 213 us; the launch traced here: 212 us
  waiting for transfers between devices  121 us (57%)
  blocking collectives  32.9 us (15%)
  matrix products  18.9 us (9%)
  local copies, waits for them, and re-layouts  18.1 us (8%)
  between operations  16 us (8%)
  other arithmetic  5 us (2%)
    psum x1, waiting for transfers between devices, body(): summed = lax.psum(local_grad, 'dp')  71.6 us
    all_gather x1, waiting for transfers between devices, body(): gathered = lax.all_gather(params, 'dp', axis=0, tiled=True)  48.9 us
    psum x1, blocking collectives, body(): losses = [lax.psum(nll_part, 'dp') / row_count]  32.9 us
    dot_general x2, matrix products, total_nll(): jnp.dot(chosen_rows, w_in, precision=lax.Precision.HIGHEST, preferred_ele...  10.4 us
    slice x2, local copies, waits for them, and re-layouts, unpack(): w_in = flat_vec[:in_end].reshape(DIN, H)  8.86 us
    dot_general x3, matrix products, total_nll(): jnp.dot(hidden, w_out, precision=lax.Precision.HIGHEST, preferred_element...  8.5 us
  transfers between devices with their start and end apart: 2, of which 2 were waited for; matrix products, arithmetic and copies ran while one was open for 2% of the time, Pallas kernels for 0%

commit v1 on v0

--- a/solution.py
+++ b/solution.py
@@ -65,7 +65,19 @@
     )
     (local_grad,) = pullback(jnp.ones_like(nll_part))
     losses = [lax.psum(nll_part, "dp") / row_count]
-    summed = lax.psum(local_grad, "dp")
+
+    def part_the_wires(chunk):
+        link_axis = "dp"
+        axis_len = lax.psum(1, link_axis)
+        b_next = chunk
+        for dd in [
+            [(q, q ^ ix) for q in range(axis_len)] for ix in (1, 2, 4, 8, 16) if ix < axis_len
+        ]:
+            next_value = lax.ppermute(b_next, link_axis, perm=dd)
+            b_next = b_next + next_value
+        return b_next
+
+    summed = part_the_wires(local_grad)
     own_grad = lax.dynamic_slice_in_dim(summed, shard_start, shard_len)
     total_force = scale_data * own_grad + precision * params
     momentum = (

time: 213 us -> 464 us (2.18); the launches traced: 212 us -> 456 us
  blocking collectives: 32.9 us -> 171 us
  waiting for transfers between devices: 121 us -> 221 us
  starting transfers between devices: 0.08 us -> 4.72 us
    ppermute x0 -> x4, waiting for transfers between devices: none -> 172 us  [part_the_wires(): next_value = lax.ppermute(b_next, link_axis, perm=dd)]
    psum x1, blocking collectives: 32.9 us -> 171 us  [body(): losses = [lax.psum(nll_part, 'dp') / row_count]]
    psum x1 -> x0, waiting for transfers between devices: 71.6 us -> none  [body(): summed = lax.psum(local_grad, 'dp')]
    ppermute x0 -> x4, starting transfers between devices: none -> 4.68 us  [part_the_wires(): next_value = lax.ppermute(b_next, link_axis, perm=dd)]
  transfers between devices with their start and end apart: 2 -> 5, of which waited for: 2 -> 4; matrix products, arithmetic and copies ran while one was open for 2% -> 1% of each run, Pallas kernels for 0% -> 0%
where the time goes in v1:
time: 464 us; the launch traced here: 456 us
  waiting for transfers between devices  221 us (48%)
  blocking collectives  171 us (37%)
  local copies, waits for them, and re-layouts  17.8 us (4%)
  matrix products  16.9 us (4%)
  between operations  16 us (3%)
  other arithmetic  9.1 us (2%)
  starting transfers between devices  4.72 us (1%)
    ppermute x4, waiting for transfers between devices, part_the_wires(): next_value = lax.ppermute(b_next, link_axis, perm=dd)  172 us
    psum x1, blocking collectives, body(): losses = [lax.psum(nll_part, 'dp') / row_count]  171 us
    all_gather x1, waiting for transfers between devices, body(): gathered = lax.all_gather(params, 'dp', axis=0, tiled=True)  48.3 us
    dot_general x2, matrix products, total_nll(): jnp.dot(chosen_rows, w_in, precision=lax.Precision.HIGHEST, preferred_ele...  9.28 us
  transfers between devices with their start and end apart: 5, of which 4 were waited for; matrix products, arithmetic and copies ran while one was open for 1% of the time, Pallas kernels for 0%

profile of v1, /device:TPU:0, one launch (start us, length us, event | category | flops | bytes accessed | tf_op | source)
XLA Modules:
  0.0 455.8 jit_solution(3389748035846653038)
XLA Ops:
  7.2 0.7 all-gather.2.cloned.1.call-update
  7.9 1.5 copy.12
  9.4 0.7 compare_select_fusion
  10.1 1.9 gather_fusion
  12.1 1.0 gather_fusion.1
  13.1 48.3 %all-gather.2.cloned.1.call-done = f32[950272]{0:T(1024)} async-done(((f32[59392]{0:T(1024)}), f32[950272]{0:T(1024)}) %all-gather.2.cloned.1.call-update) | async-done | bytes 3801104 | tf_op jit(solution)/shard_map/all_gather | solution.py:59
  61.4 4.1 slice.31
  65.5 4.8 %slice.23 = f32[448,2048]{1,0:T(8,128)} reshape(f32[917504]{0:T(1024)} %slice.31) | data formatting | bytes 7340032 | tf_op jit(solution)/shard_map/jvp()/slice | solution.py:16
  70.3 1.0 reshape.81
  71.3 5.7 %fusion = f32[256,2048]{1,0:T(8,128)S(1)} fusion(f32[448,2048]{1,0:T(8,128)} %slice.23, f32[2048]{0:T(1024)S(1)} %slice-done.1, f32[256,448]{1,0:T(8,128)S(1)} %gather_fusion.1, pred[256]{0:T(512)(128)(4,1)S(1)} %get-tuple-element.8), kind=kOutput, calls=%fused_computation.4 | convolution fusion | flops 2819211264 | bytes 6234368 | tf_op jit(solution)/shard_map/jvp()/dot_general | solution.py:27
  77.1 1.9 exponential_reduce_fusion
  78.9 2.1 fusion.25
  81.1 3.6 fusion.15
  84.7 0.1 select_reduce_fusion
  84.8 3.6 convolution_bitcast_fusion
  88.4 2.6 copy.15
  91.0 0.8 reshape.82
  91.7 2.4 pad_add_fusion
  94.2 0.3 collective-permute-start
  94.5 6.4 %collective-permute-done = f32[950272]{0:T(1024)S(1)} collective-permute-done((f32[950272]{0:T(1024)S(1)}, f32[950272]{0:T(1024)S(1)}, u32[]{:S(2)}, u32[]{:S(2)}) %collective-permute-start) | collective-permute-done | bytes 3801120 | tf_op jit(solution)/shard_map/ppermute | solution.py:76
  100.8 0.4 fusion.23
  101.2 0.6 collective-permute-start.1
  101.9 83.7 %collective-permute-done.1 = f32[950272]{0:T(1024)S(1)} collective-permute-done((f32[950272]{0:T(1024)S(1)}, f32[950272]{0:T(1024)S(1)}, u32[]{:S(2)}, u32[]{:S(2)}) %collective-permute-start.1) | collective-permute-done | bytes 3801120 | tf_op jit(solution)/shard_map/ppermute | solution.py:76
  185.6 0.4 add.97
  186.0 1.8 collective-permute-start.2
  187.8 81.7 %collective-permute-done.2 = f32[950272]{0:T(1024)S(1)} collective-permute-done((f32[950272]{0:T(1024)S(1)}, f32[950272]{0:T(1024)S(1)}, u32[]{:S(2)}, u32[]{:S(2)}) %collective-permute-start.2) | collective-permute-done | bytes 3801120 | tf_op jit(solution)/shard_map/ppermute | solution.py:76
  269.5 2.2 add.98
  271.7 2.0 collective-permute-start.3
  273.7 0.2 broadcast_multiply_fusion
  274.0 0.6 subtract_reduce_fusion
  274.6 170.6 %psum.7 = f32[]{:T(128)} all-reduce(f32[]{:T(128)} %subtract_reduce_fusion), channel_id=1, replica_groups=mesh['grp'=2,'dp'=16] {'dp'}, use_global_device_ids=true, to_apply=%region_5.6 | all-reduce | flops 1 | bytes 8 | tf_op jit(solution)/shard_map/psum | solution.py:67
  445.9 2.0 multiply_add_fusion
  (23 shorter events, 0.1 us)
Async XLA Ops:
  7.2 3.0 copy-start
  7.2 54.2 %all-gather.2.cloned.1.call-start = ((), (), s32[]{:S(2)}) async-start(), calls=%async_computation | async-start | bytes 4038656 | tf_op jit(solution)/shard_map/all_gather | solution.py:59
  7.9 5.2 %copy-start.5 = (s32[1,256]{1,0:T(1,128)S(1)}, s32[1,256]{1,0:T(1,128)}, u32[]{:S(2)}) copy-start(s32[1,256]{1,0:T(1,128)} %param.11) | copy-start | bytes 3076
  65.5 4.8 %slice-start = ((f32[950272]{0:T(1024)}), f32[20480]{0:T(1024)S(1)}, s32[]{:S(2)}) async-start(f32[950272]{0:T(1024)} %all-gather.2.cloned.1.call-done), calls=%async_computation.1 | async-start | bytes 163840 | tf_op jit(solution)/shard_map/jvp()/slice | solution.py:19
  65.5 5.8 %slice-start.1 = ((f32[950272]{0:T(1024)}), f32[2048]{0:T(1024)S(1)}, s32[]{:S(2)}) async-start(f32[950272]{0:T(1024)} %all-gather.2.cloned.1.call-done), calls=%async_computation.2 | async-start | bytes 16384 | tf_op jit(solution)/shard_map/jvp()/slice | solution.py:17
  70.3 6.8 %slice-start.2 = ((f32[950272]{0:T(1024)}), f32[10]{0:T(128)S(1)}, s32[]{:S(2)}) async-start(f32[950272]{0:T(1024)} %all-gather.2.cloned.1.call-done), calls=%async_computation.3 | async-start | bytes 1024 | tf_op jit(solution)/shard_map/jvp()/slice | solution.py:20
  91.7 9.1 %copy-start.1 = (f32[56,16,8,128]{3,1,2,0:T(8,128)S(1)}, f32[56,16,8,128]{3,1,2,0:T(8,128)}, u32[]{:S(2)}) copy-start(f32[56,16,8,128]{3,1,2,0:T(8,128)} %copy.15) | copy-start | bytes 11010052
  94.2 6.7 %collective-permute-start = (f32[950272]{0:T(1024)S(1)}, f32[950272]{0:T(1024)S(1)}, u32[]{:S(2)}, u32[]{:S(2)}) collective-permute-start(f32[950272]{0:T(1024)S(1)} %pad_add_fusion), channel_id=1, source_target_pairs={{0,1},{1,0},{2,3},{3,2},{4,5},{5,4},{6,7},{7,6},{8,9},{9,8},{10,11... | collective-permute-start | bytes 11403272 | tf_op jit(solution)/shard_map/ppermute | solution.py:76
  101.2 84.4 %collective-permute-start.1 = (f32[950272]{0:T(1024)S(1)}, f32[950272]{0:T(1024)S(1)}, u32[]{:S(2)}, u32[]{:S(2)}) collective-permute-start(f32[950272]{0:T(1024)S(1)} %fusion.23), channel_id=1, source_target_pairs={{0,2},{1,3},{2,0},{3,1},{4,6},{5,7},{6,4},{7,5},{8,10},{9,11},{10,... | collective-permute-start | bytes 11403272 | tf_op jit(solution)/shard_map/ppermute | solution.py:76
  186.0 87.7 %copy-start.3 = (f32[1,59392]{1,0:T(1,128)S(1)}, f32[1,59392]{1,0:T(1,128)}, u32[]{:S(2)}) copy-start(f32[1,59392]{1,0:T(1,128)} %param.8) | copy-start | bytes 712708
  186.0 259.9 %copy-start.2 = (f32[59392]{0:T(1024)S(1)}, f32[59392]{0:T(1024)}, u32[]{:S(2)}) copy-start(f32[59392]{0:T(1024)} %param.6) | copy-start | bytes 712708
  186.0 259.9 %copy-start.4 = (f32[59392]{0:T(1024)S(1)}, f32[59392]{0:T(1024)}, u32[]{:S(2)}) copy-start(f32[59392]{0:T(1024)} %param.7) | copy-start | bytes 712708
  186.0 83.5 %collective-permute-start.2 = (f32[950272]{0:T(1024)S(1)}, f32[950272]{0:T(1024)S(1)}, u32[]{:S(2)}, u32[]{:S(2)}) collective-permute-start(f32[950272]{0:T(1024)S(1)} %add.97), channel_id=1, source_target_pairs={{0,4},{1,5},{2,6},{3,7},{4,0},{5,1},{6,2},{7,3},{8,12},{9,13},{10,... | collective-permute-start | bytes 11403272 | tf_op jit(solution)/shard_map/ppermute | solution.py:76
  271.7 174.1 %collective-permute-start.3 = (f32[950272]{0:T(1024)}, f32[950272]{0:T(1024)}, u32[]{:S(2)}, u32[]{:S(2)}) collective-permute-start(f32[950272]{0:T(1024)} %add.98), channel_id=1, source_target_pairs={{0,8},{1,9},{2,10},{3,11},{4,12},{5,13},{6,14},{7,15},{8,0},{9,1},... | collective-permute-start | bytes 11403272 | tf_op jit(solution)/shard_map/ppermute | solution.py:76
Sparse Core Ops, SparseCore 0:
  10.3 51.0 all-gather.1
